TPU v7x, 512 devices: a whole 4x4x16 slice. The times are simulated.
512 devices in a mesh: seq: 32 (over z, y_lo), tp: 16 (over x, y_hi, core).
Axes of the slice: x: 4, y: 4 (y_hi: 2, y_lo: 2; y = y_hi * 2 + y_lo), z: 16, core: 2. Of those that a mesh axis runs over, the one named last changes fastest.
Arguments:
- inputs: bfloat16 [2, 128, 8192], P(None, 'seq', 'tp'), may hold values from -6 to 6
- out_grad: bfloat16 [2, 128, 8192], P(None, 'seq', 'tp'), may hold values from -6 to 6
- gate_weight: bfloat16 [8192, 14848], P('tp', 'seq'), may hold values from -0.0625 to 0.0625
- up_weight: bfloat16 [8192, 14848], P('tp', 'seq'), may hold values from -0.0625 to 0.0625
- down_weight: bfloat16 [14848, 8192], P('seq', 'tp'), may hold values from -0.0625 to 0.0625
Outputs:
- input_grad: bfloat16 [2, 128, 8192], P(None, 'seq', 'tp')
- gate_grad: float32 [8192, 14848], P('tp', 'seq')
- up_grad: float32 [8192, 14848], P('tp', 'seq')
- down_grad: float32 [14848, 8192], P('seq', 'tp')
All inputs are finite; a program needn't handle non-finite values.
Results may differ from a plain program's by a relative error of at most 0.0049.
Values may be sent and summed in bfloat16 or wider, within the bound.
A program may use at most 64 MiB of HBM per device.

v0:
```python
import jax
import jax.numpy as jnp
from jax import lax
from jax.sharding import Mesh
from jax.sharding import PartitionSpec as P

TP = ("tp_0", "tp_1", "tp_2")


def from_everyone(value, axis):
    count = lax.axis_size(axis)
    return lax.all_to_all(
        jnp.broadcast_to(value[None], (count, *value.shape)), axis, 0, 0, tiled=True
    )


def laid_out(blocks, dim):
    lengths = list(blocks.shape[1:])
    lengths[dim] *= blocks.shape[0]
    return jnp.moveaxis(blocks, 0, dim).reshape(lengths)


def collect(value, axis, dim):
    blocks = from_everyone(value, axis)
    return laid_out(blocks, dim)


def side_by_side(arrays, axis, dim, along):
    widths = [a.shape[along] for a in arrays]
    both = jnp.concatenate(arrays, axis=along)
    result = collect(both, axis, dim)
    return tuple(jnp.split(result, [sum(widths[:k]) for k in range(1, len(widths))], axis=along))


def cut_along(value, dim, count):
    lengths = value.shape
    blocks = value.reshape(*lengths[:dim], count, lengths[dim] // count, *lengths[dim + 1 :])
    return jnp.moveaxis(blocks, dim, 0)


def sum_at_owner(value, axis, dim):
    blocks = cut_along(value, dim, lax.axis_size(axis))
    arrived = lax.all_to_all(blocks, axis, split_axis=0, concat_axis=0, tiled=True)
    return arrived.sum(axis=0)


def in_one_piece(arrays, axis, dim, along):
    widths = [a.shape[along] for a in arrays]
    both = jnp.concatenate(arrays, axis=along)
    result = lax.all_gather(both, axis, axis=dim, tiled=True)
    return tuple(jnp.split(result, [sum(widths[:k]) for k in range(1, len(widths))], axis=along))


def rows_for(lines, count):
    spare = -len(lines) % count
    return jnp.pad(lines, [(0, spare)] + [(0, 0)] * (lines.ndim - 1))


def gathered_by_axis(value, axes, dim):
    far, near = axes
    first = from_everyone(value, far)
    blocks = jnp.swapaxes(from_everyone(first, near), 0, 1)
    return laid_out(blocks.reshape(-1, *value.shape), dim)


def sum_by_axis(value, axes, dim):
    far, near = axes
    own = sum_at_owner(cut_along(value, dim, lax.axis_size(far)), near, dim + 1)
    return jnp.sum(lax.all_to_all(own, far, 0, 0, tiled=True), axis=0)


def total_of(value, axes):
    padded = rows_for(value, lax.axis_size(axes[0]) * lax.axis_size(axes[1]))
    whole = gathered_by_axis(sum_by_axis(padded, axes, 0), axes, 0)
    return lax.slice_in_dim(whole, 0, len(value)).reshape(value.shape)


def together(arrays, axis):
    ravelled, at, finished = (jnp.concatenate([a.reshape(-1) for a in arrays]), 0, [])
    total = total_of(ravelled, axis)
    for a in arrays:
        finished.append(total[at : at + a.size].reshape(a.shape))
        at += a.size
    return tuple(finished)


def per_device(inputs, out_grad, gate_weight, up_weight, down_weight):
    blocks = inputs.shape[0]
    local_rows = inputs.shape[1]
    width_count = lax.axis_size(TP)
    block_tokens = local_rows * lax.axis_size("seq")
    share_rows = block_tokens // width_count
    share_start = lax.axis_index(TP) * share_rows
    contract_first = (((0,), (0,)), ((), ()))
    contract_last = (((1,), (1,)), ((), ()))

    def token_block(index):
        return side_by_side((inputs[index], out_grad[index]), "seq", 0, 1)

    def forward_terms(whole_in):
        gate_part = jnp.dot(whole_in, gate_weight, preferred_element_type=jnp.float32)
        up_part = jnp.dot(whole_in, up_weight, preferred_element_type=jnp.float32)
        return (gate_part, up_part)

    gathered = [token_block(index) for index in range(blocks)]
    partials = [forward_terms(pair[0]) for pair in gathered]
    gate_all, up_all = together(
        (jnp.stack([item[0] for item in partials]), jnp.stack([item[1] for item in partials])),
        (("tp_0", "tp_1"), "tp_2"),
    )
    totals = None
    results = [None] * blocks
    for index in range(blocks):
        whole_in, whole_grad = gathered[index]
        gate, up_proj = (gate_all[index], up_all[index])
        hidden_share = sum_at_owner(
            lax.dot_general(
                whole_grad, down_weight, contract_last, preferred_element_type=jnp.float32
            ),
            TP,
            0,
        )
        gate_share = lax.dynamic_slice_in_dim(gate, share_start, share_rows, 0)
        up_share = lax.dynamic_slice_in_dim(up_proj, share_start, share_rows, 0)
        sig = jax.nn.sigmoid(gate_share)
        up_local = (hidden_share * gate_share * sig).astype(jnp.bfloat16)
        gate_local = (hidden_share * up_share * sig * (1.0 + gate_share * (1.0 - sig))).astype(
            jnp.bfloat16
        )
        front_unit_gate, front_unit_up = in_one_piece((gate_local, up_local), TP, 0, 1)
        hidden = (jax.nn.silu(gate) * up_proj).astype(jnp.bfloat16)
        down_term = lax.dot_general(
            hidden, whole_grad, contract_first, preferred_element_type=jnp.float32
        )
        gate_term = lax.dot_general(
            whole_in, front_unit_gate, contract_first, preferred_element_type=jnp.float32
        )
        up_term = lax.dot_general(
            whole_in, front_unit_up, contract_first, preferred_element_type=jnp.float32
        )
        terms = (gate_term, up_term, down_term)
        if totals is None:
            totals = terms
        else:
            totals = (totals[0] + terms[0], totals[1] + terms[1], totals[2] + terms[2])
        first = lax.dot_general(
            front_unit_gate, gate_weight, contract_last, preferred_element_type=jnp.float32
        )
        second = lax.dot_general(
            front_unit_up, up_weight, contract_last, preferred_element_type=jnp.float32
        )
        results[index] = sum_at_owner(first + second, "seq", 0).astype(jnp.bfloat16)
    return (jnp.stack(results), totals[0], totals[1], totals[2])


def solution(mesh):
    finer = Mesh(mesh.devices.reshape(mesh.shape["seq"], 4, 2, 2), ("seq", "tp_0", "tp_1", "tp_2"))
    in_specs = (P(None, "seq", TP), P(None, "seq", TP), P(TP, "seq"), P(TP, "seq"), P("seq", TP))
    out_specs = (P(None, "seq", TP), P(TP, "seq"), P(TP, "seq"), P("seq", TP))
    return jax.shard_map(
        per_device, mesh=finer, in_specs=in_specs, out_specs=out_specs, check_vma=False
    )
```

profile of v0, /device:TPU:1, one launch (start us, length us, event | category | flops | bytes accessed | tf_op | source)
XLA Modules:
  0.0 241.2 jit_solution(736752744043739455)
XLA Ops:
  2.2 17.0 %all-to-all-start = ((bf16[32,4,1024]{2,1,0:T(4,128)(2,1)}), bf16[32,4,1024]{2,1,0:T(4,128)(2,1)S(1)}, u32[]{:S(2)}, u32[]{:S(2)}) async-start(bf16[32,4,1024]{2,1,0:T(4,128)(2,1)} %broadcast_in_dim.10), calls=%async_computation | async-start | bytes 524288 | tf_op jit(solution)/shard_map/all_to_all | solution.py:12
  19.3 20.4 %all-to-all-done = bf16[32,4,1024]{2,1,0:T(4,128)(2,1)S(1)} async-done(((bf16[32,4,1024]{2,1,0:T(4,128)(2,1)}), bf16[32,4,1024]{2,1,0:T(4,128)(2,1)S(1)}, u32[]{:S(2)}, u32[]{:S(2)}) %all-to-all-start) | async-done | bytes 262176 | tf_op jit(solution)/shard_map/all_to_all | solution.py:12
  40.4 4.0 %all-to-all-start.2 = ((bf16[32,4,1024]{2,1,0:T(4,128)(2,1)}), bf16[32,4,1024]{2,1,0:T(4,128)(2,1)S(1)}, u32[]{:S(2)}, u32[]{:S(2)}) async-start(bf16[32,4,1024]{2,1,0:T(4,128)(2,1)} %broadcast_in_dim.11), calls=%async_computation.2 | async-start | bytes 524288 | tf_op jit(solution)/shard_map/all_to_all | solution.py:12
  44.9 18.6 %all-to-all-done.2 = bf16[32,4,1024]{2,1,0:T(4,128)(2,1)S(1)} async-done(((bf16[32,4,1024]{2,1,0:T(4,128)(2,1)}), bf16[32,4,1024]{2,1,0:T(4,128)(2,1)S(1)}, u32[]{:S(2)}, u32[]{:S(2)}) %all-to-all-start.2) | async-done | bytes 262176 | tf_op jit(solution)/shard_map/all_to_all | solution.py:12
  67.3 1.1 copy.16
  68.4 7.6 %all-to-all-start.3 = ((f32[2,8,14848]{2,1,0:T(8,128)}), f32[2,8,14848]{2,1,0:T(8,128)S(1)}, u32[]{:S(2)}, u32[]{:S(2)}) async-start(f32[2,8,14848]{2,1,0:T(8,128)} %copy.16), calls=%async_computation.3 | async-start | bytes 1900544 | tf_op jit(solution)/shard_map/all_to_all | solution.py:43
  77.7 7.0 %all-to-all-start.1 = ((f32[16,8,464]{2,1,0:T(8,128)}), f32[16,8,464]{2,1,0:T(8,128)}, u32[]{:S(2)}, u32[]{:S(2)}) async-start(f32[16,8,464]{2,1,0:T(8,128)} %convolution_bitcast_fusion.1), calls=%async_computation.1 | async-start | bytes 524288 | tf_op jit(solution)/shard_map/all_to_all | solution.py:43
  85.9 7.8 %all-to-all-done.1 = f32[16,8,464]{2,1,0:T(8,128)} async-done(((f32[16,8,464]{2,1,0:T(8,128)}), f32[16,8,464]{2,1,0:T(8,128)}, u32[]{:S(2)}, u32[]{:S(2)}) %all-to-all-start.1) | async-done | bytes 237600 | tf_op jit(solution)/shard_map/all_to_all | solution.py:43
  93.7 3.5 %all-to-all-start.4 = ((f32[8,1,14848]{2,1,0:T(1,128)}), f32[8,1,14848]{2,1,0:T(1,128)S(1)}, u32[]{:S(2)}, u32[]{:S(2)}) async-start(f32[8,1,14848]{2,1,0:T(1,128)} %all_to_all.38), calls=%async_computation.4 | async-start | bytes 950272 | tf_op jit(solution)/shard_map/all_to_all | solution.py:69
  98.2 9.1 %all-to-all-done.4 = f32[8,1,14848]{2,1,0:T(1,128)S(1)} async-done(((f32[8,1,14848]{2,1,0:T(1,128)}), f32[8,1,14848]{2,1,0:T(1,128)S(1)}, u32[]{:S(2)}, u32[]{:S(2)}) %all-to-all-start.4) | async-done | bytes 475168 | tf_op jit(solution)/shard_map/all_to_all | solution.py:69
  107.3 4.6 %all-to-all-start.8 = ((f32[16,8,464]{2,1,0:T(8,128)}), f32[16,8,464]{2,1,0:T(8,128)S(1)}, u32[]{:S(2)}, u32[]{:S(2)}) async-start(f32[16,8,464]{2,1,0:T(8,128)} %convolution_bitcast_fusion), calls=%async_computation.8 | async-start | bytes 524288 | tf_op jit(solution)/shard_map/all_to_all | solution.py:43
  112.2 8.5 %all-to-all-done.8 = f32[16,8,464]{2,1,0:T(8,128)S(1)} async-done(((f32[16,8,464]{2,1,0:T(8,128)}), f32[16,8,464]{2,1,0:T(8,128)S(1)}, u32[]{:S(2)}, u32[]{:S(2)}) %all-to-all-start.8) | async-done | bytes 237600 | tf_op jit(solution)/shard_map/all_to_all | solution.py:43
  121.8 3.5 %all-to-all-start.5 = ((f32[8,1,14848]{2,1,0:T(1,128)}), f32[8,1,14848]{2,1,0:T(1,128)S(1)}, u32[]{:S(2)}, u32[]{:S(2)}) async-start(f32[8,1,14848]{2,1,0:T(1,128)} %broadcast_in_dim.12), calls=%async_computation.5 | async-start | bytes 950272 | tf_op jit(solution)/shard_map/all_to_all | solution.py:12
  126.3 9.1 %all-to-all-done.5 = f32[8,1,14848]{2,1,0:T(1,128)S(1)} async-done(((f32[8,1,14848]{2,1,0:T(1,128)}), f32[8,1,14848]{2,1,0:T(1,128)S(1)}, u32[]{:S(2)}, u32[]{:S(2)}) %all-to-all-start.5) | async-done | bytes 475168 | tf_op jit(solution)/shard_map/all_to_all | solution.py:12
  135.5 5.3 %all_to_all.55 = f32[2,8,14848]{2,1,0:T(8,128)S(1)} all-to-all(f32[2,8,14848]{2,1,0:T(8,128)S(1)} %broadcast_in_dim.14), channel_id=1, replica_groups=mesh['seq'=32,'tp_0'=4,'tp_1'=2,'tp_2'=2] {'tp_2'}, dimensions={0} | all-to-all | bytes 1900544 | tf_op jit(solution)/shard_map/all_to_all | solution.py:12
  143.2 22.0 %all_gather.6 = bf16[128,928]{1,0:T(8,128)(2,1)S(1)} all-gather(bf16[8,928]{1,0:T(8,128)(2,1)S(1)} %pad_maximum_fusion.2), channel_id=1, replica_groups=mesh['seq'=32,'tp_0'=4,'tp_1'=2,'tp_2'=2] {'tp_0','tp_1','tp_2'}, dimensions={0}, use_global_device_ids=true | all-gather | bytes 252416 | tf_op jit(solution)/shard_map/all_gather | solution.py:50
  165.2 21.0 %all_gather.7 = bf16[128,928]{1,0:T(8,128)(2,1)S(1)} all-gather(bf16[8,928]{1,0:T(8,128)(2,1)S(1)} %pad_maximum_fusion.3), channel_id=1, replica_groups=mesh['seq'=32,'tp_0'=4,'tp_1'=2,'tp_2'=2] {'tp_0','tp_1','tp_2'}, dimensions={0}, use_global_device_ids=true | all-gather | bytes 252416 | tf_op jit(solution)/shard_map/all_gather | solution.py:50
  187.6 4.6 %all-to-all-start.7 = ((f32[32,4,512]{2,1,0:T(4,128)}), f32[32,4,512]{2,1,0:T(4,128)}, u32[]{:S(2)}, u32[]{:S(2)}) async-start(f32[32,4,512]{2,1,0:T(4,128)} %reshape.77), calls=%async_computation.7 | async-start | bytes 524288 | tf_op jit(solution)/shard_map/all_to_all | solution.py:43
  194.8 19.3 %all-to-all-done.7 = f32[32,4,512]{2,1,0:T(4,128)} async-done(((f32[32,4,512]{2,1,0:T(4,128)}), f32[32,4,512]{2,1,0:T(4,128)}, u32[]{:S(2)}, u32[]{:S(2)}) %all-to-all-start.7) | async-done | bytes 262176 | tf_op jit(solution)/shard_map/all_to_all | solution.py:43
  214.1 4.6 %all-to-all-start.9 = ((f32[32,4,512]{2,1,0:T(4,128)}), f32[32,4,512]{2,1,0:T(4,128)}, u32[]{:S(2)}, u32[]{:S(2)}) async-start(f32[32,4,512]{2,1,0:T(4,128)} %reshape.79), calls=%async_computation.9 | async-start | bytes 524288 | tf_op jit(solution)/shard_map/all_to_all | solution.py:43
  219.7 1.4 convolution_add_fusion.1
  221.0 1.3 convolution_add_fusion.2
  222.3 1.3 convolution_add_fusion
  224.6 15.0 %all-to-all-done.9 = f32[32,4,512]{2,1,0:T(4,128)} async-done(((f32[32,4,512]{2,1,0:T(4,128)}), f32[32,4,512]{2,1,0:T(4,128)}, u32[]{:S(2)}, u32[]{:S(2)}) %all-to-all-start.9) | async-done | bytes 262176 | tf_op jit(solution)/shard_map/all_to_all | solution.py:43
  (84 shorter events, 22.8 us)
Async XLA Ops:
  0.6 43.9 %copy-start = (bf16[512,464]{0,1:T(8,128)(2,1)S(1)}, bf16[512,464]{0,1:T(8,128)(2,1)}, u32[]{:S(2)}) copy-start(bf16[512,464]{0,1:T(8,128)(2,1)} %param.7) | copy-start | bytes 1425412
  2.2 37.4 %all-to-all-start = ((bf16[32,4,1024]{2,1,0:T(4,128)(2,1)}), bf16[32,4,1024]{2,1,0:T(4,128)(2,1)S(1)}, u32[]{:S(2)}, u32[]{:S(2)}) async-start(bf16[32,4,1024]{2,1,0:T(4,128)(2,1)} %broadcast_in_dim.10), calls=%async_computation | async-start | bytes 524288 | tf_op jit(solution)/shard_map/all_to_all | solution.py:12
  40.4 23.0 %all-to-all-start.2 = ((bf16[32,4,1024]{2,1,0:T(4,128)(2,1)}), bf16[32,4,1024]{2,1,0:T(4,128)(2,1)S(1)}, u32[]{:S(2)}, u32[]{:S(2)}) async-start(bf16[32,4,1024]{2,1,0:T(4,128)(2,1)} %broadcast_in_dim.11), calls=%async_computation.2 | async-start | bytes 524288 | tf_op jit(solution)/shard_map/all_to_all | solution.py:12
  63.5 1.0 copy-start.1
  68.4 7.6 %copy-start.6 = (bf16[464,512]{1,0:T(8,128)(2,1)S(1)}, bf16[464,512]{1,0:T(8,128)(2,1)}, u32[]{:S(2)}) copy-start(bf16[464,512]{1,0:T(8,128)(2,1)} %param.9) | copy-start | bytes 1425412
  68.4 9.3 %all-to-all-start.3 = ((f32[2,8,14848]{2,1,0:T(8,128)}), f32[2,8,14848]{2,1,0:T(8,128)S(1)}, u32[]{:S(2)}, u32[]{:S(2)}) async-start(f32[2,8,14848]{2,1,0:T(8,128)} %copy.16), calls=%async_computation.3 | async-start | bytes 1900544 | tf_op jit(solution)/shard_map/all_to_all | solution.py:43
  77.7 16.0 %all-to-all-start.1 = ((f32[16,8,464]{2,1,0:T(8,128)}), f32[16,8,464]{2,1,0:T(8,128)}, u32[]{:S(2)}, u32[]{:S(2)}) async-start(f32[16,8,464]{2,1,0:T(8,128)} %convolution_bitcast_fusion.1), calls=%async_computation.1 | async-start | bytes 524288 | tf_op jit(solution)/shard_map/all_to_all | solution.py:43
  93.7 13.6 %all-to-all-start.4 = ((f32[8,1,14848]{2,1,0:T(1,128)}), f32[8,1,14848]{2,1,0:T(1,128)S(1)}, u32[]{:S(2)}, u32[]{:S(2)}) async-start(f32[8,1,14848]{2,1,0:T(1,128)} %all_to_all.38), calls=%async_computation.4 | async-start | bytes 950272 | tf_op jit(solution)/shard_map/all_to_all | solution.py:69
  107.3 13.4 %all-to-all-start.8 = ((f32[16,8,464]{2,1,0:T(8,128)}), f32[16,8,464]{2,1,0:T(8,128)S(1)}, u32[]{:S(2)}, u32[]{:S(2)}) async-start(f32[16,8,464]{2,1,0:T(8,128)} %convolution_bitcast_fusion), calls=%async_computation.8 | async-start | bytes 524288 | tf_op jit(solution)/shard_map/all_to_all | solution.py:43
  121.8 13.6 %all-to-all-start.5 = ((f32[8,1,14848]{2,1,0:T(1,128)}), f32[8,1,14848]{2,1,0:T(1,128)S(1)}, u32[]{:S(2)}, u32[]{:S(2)}) async-start(f32[8,1,14848]{2,1,0:T(1,128)} %broadcast_in_dim.12), calls=%async_computation.5 | async-start | bytes 950272 | tf_op jit(solution)/shard_map/all_to_all | solution.py:12
  141.5 1.5 copy-start.11
  142.0 1.0 copy-start.13
  142.5 22.6 %copy-start.7 = (f32[128,464]{1,0:T(8,128)}, f32[128,464]{1,0:T(8,128)S(1)}, u32[]{:S(2)}) copy-start(f32[128,464]{1,0:T(8,128)S(1)} %squeeze.30) | copy-start | bytes 712708
  143.1 43.2 %copy-start.9 = (f32[128,464]{1,0:T(8,128)}, f32[128,464]{1,0:T(8,128)S(1)}, u32[]{:S(2)}) copy-start(f32[128,464]{1,0:T(8,128)S(1)} %squeeze.31) | copy-start | bytes 712708
  165.1 28.3 %copy-start.2 = (bf16[128,928]{1,0:T(8,128)(2,1)}, bf16[128,928]{1,0:T(8,128)(2,1)S(1)}, u32[]{:S(2)}) copy-start(bf16[128,928]{1,0:T(8,128)(2,1)S(1)} %all_gather.6) | copy-start | bytes 712708
  186.3 6.1 %copy-start.4 = (bf16[128,928]{1,0:T(8,128)(2,1)}, bf16[128,928]{1,0:T(8,128)(2,1)S(1)}, u32[]{:S(2)}) copy-start(bf16[128,928]{1,0:T(8,128)(2,1)S(1)} %all_gather.7) | copy-start | bytes 712708
  187.6 26.5 %all-to-all-start.7 = ((f32[32,4,512]{2,1,0:T(4,128)}), f32[32,4,512]{2,1,0:T(4,128)}, u32[]{:S(2)}, u32[]{:S(2)}) async-start(f32[32,4,512]{2,1,0:T(4,128)} %reshape.77), calls=%async_computation.7 | async-start | bytes 524288 | tf_op jit(solution)/shard_map/all_to_all | solution.py:43
  193.4 1.0 copy-start.12
  193.4 1.0 copy-start.14
  194.8 23.9 %copy-start.3 = (bf16[128,928]{1,0:T(8,128)(2,1)S(1)}, bf16[128,928]{1,0:T(8,128)(2,1)}, u32[]{:S(2)}) copy-start(bf16[128,928]{1,0:T(8,128)(2,1)} %copy-done.2) | copy-start | bytes 712708
  214.1 25.4 %all-to-all-start.9 = ((f32[32,4,512]{2,1,0:T(4,128)}), f32[32,4,512]{2,1,0:T(4,128)}, u32[]{:S(2)}, u32[]{:S(2)}) async-start(f32[32,4,512]{2,1,0:T(4,128)} %reshape.79), calls=%async_computation.9 | async-start | bytes 524288 | tf_op jit(solution)/shard_map/all_to_all | solution.py:43
  218.7 1.0 copy-start.5
  221.0 1.3 copy-start.8
  221.0 1.3 copy-start.10
where the time goes:
time: 243 us; the launch traced here: 241 us
  waiting for transfers between devices  108 us (44%)
  starting transfers between devices  56.4 us (23%)
  blocking collectives  48.2 us (20%)
  local copies, waits for them, and re-layouts  13.3 us (5%)
  matrix products  9.02 us (4%)
  other arithmetic  4.74 us (2%)
    all_to_all x5, waiting for transfers between devices, sum_at_owner(): lax.all_to_all(blocks, axis, split_axis=0, concat_axis=0, tiled=True)  51.3 us
    all_to_all x3, waiting for transfers between devices, from_everyone(): lax.all_to_all(jnp.broadcast_to(value[None], (count, *value.shape)), axis...  48 us
    all_gather x2, blocking collectives, in_one_piece(): result = lax.all_gather(both, axis, axis=dim, tiled=True)  43 us
    all_to_all x5, starting transfers between devices, sum_at_owner(): lax.all_to_all(blocks, axis, split_axis=0, concat_axis=0, tiled=True)  28.4 us
    all_to_all x3, starting transfers between devices, from_everyone(): lax.all_to_all(jnp.broadcast_to(value[None], (count, *value.shape)), axis...  24.5 us
    all_to_all x1, waiting for transfers between devices, sum_by_axis(): return jnp.sum(lax.all_to_all(own, far, 0, 0, tiled=True), axis=0)  9.11 us
    all_to_all x1, blocking collectives, from_everyone(): lax.all_to_all(jnp.broadcast_to(value[None], (count, *value.shape)), axis...  5.26 us
  transfers between devices with their start and end apart: 9, of which 9 were waited for; matrix products, arithmetic and copies ran while one was open for 5% of the time, Pallas kernels for 0%

commit v1 on v0

v1 whole, which is shorter than its diff:
```python
import jax
import jax.numpy as jnp
from jax import lax
from jax.experimental import pallas as pl
from jax.experimental.pallas import tpu as pltpu
from jax.sharding import PartitionSpec as P

MESH = pl.DeviceIdType.MESH
F32, BF16 = jnp.float32, jnp.bfloat16

SPREAD = {0: (3, -3, 1, -1), -3: (3, 1, -1), 3: (-3, -1, 1), -6: (2, 1, -1), 6: (-2, -1, 1)}
LABELS = (-1, 1, -3, 3, -4, -2, 2, 4, -6, 6, -7, -5, 5, 7, -8, 8)
PARENT = {1: 0, -1: 0, 2: 3, 4: 3, -2: -3, -4: -3, 5: 6, 7: 6, -5: -6, -7: -6, 8: 6, -8: -6,
          6: 3, -6: -3, 3: 0, -3: 0}
LEAVES = (8, -8, 7, -7, 5, -5, 4, -4, 2, -2, 1, -1)
CHILDREN = {6: (5, 7, 8), -6: (-5, -7, -8), 3: (2, 4, 6), -3: (-2, -4, -6), 0: (1, -1, 3, -3)}
Y_ORDER = (8, 7, -7, 5, -5, 6, -6, 4, -4, 2, -2, 3, -3, 1, -1, 0)


def kernel(nz, nx, x_ref, dy_ref, wg_any, wu_any, wd_any, dx_ref, gg_any, ug_any, dg_any,
           buf, wg, wu, wd, xs, ys, own, far, got, slabs, landed, act,
           dxp, ysend, yrecv, zsend, zrecv, gg, ug, dg,
           load_sem, store_sem, zs_sem, zr_sem, ys_sem, yr_sem, cs_sem, cr_sem,
           ts_sem, tr_sem, as_sem, ar_sem, bs_sem, br_sem, fys_sem, fyr_sem, fzs_sem, fzr_sem):
    s = lax.axis_index("seq")
    t = lax.axis_index("tp")
    z, yl = s // 2, s % 2
    core, yh, x = t % 2, (t // 2) % 2, t // 4

    def seq_at(dz, flip=0):
        return lax.rem(z + dz + nz, nz) * 2 + (yl if flip == 0 else 1 - yl)

    def chip_at(dx, dyh):
        return lax.rem(x + dx + nx, nx) * 2 + lax.rem(yh + dyh, 2)

    others = [(2, 1), (1, 1), (3, 1), (2, 0), (0, 1), (1, 0), (3, 0)]

    def copy_to(src, dst, send, recv, device):
        return pltpu.make_async_remote_copy(
            src_ref=src, dst_ref=dst, send_sem=send, recv_sem=recv, device_id=device,
            device_id_type=MESH)

    mate = (s, t + 1 - 2 * core)
    across = (seq_at(0, 1), t)
    barrier = pltpu.get_barrier_semaphore()
    partners = [(seq_at(d), t) for d in (3, -3, 2, -2, 1, -1)] + [across, mate]
    partners += [(s, chip_at(*k) * 2 + core) for k in others]
    for device in partners:
        pl.semaphore_signal(barrier, inc=1, device_id=device, device_id_type=MESH)
    loads = [pltpu.make_async_copy(a, b, load_sem.at[i])
             for i, (a, b) in enumerate(((wg_any, wg), (wu_any, wu), (wd_any, wd)))]
    for c in loads:
        c.start()
    rows, depth = buf.shape[2], buf.shape[3]
    buf[s, 0] = x_ref[...].reshape(rows, depth)
    buf[s, 1] = dy_ref[...].reshape(rows, depth)
    pl.semaphore_wait(barrier, len(partners))

    sent = []

    def send(*a):
        c = copy_to(*a)
        c.start()
        sent.append(c)

    def part(o, label):
        ref = buf.at[seq_at(o)]
        if label == -8:
            return ref.at[0]
        if label == 8:
            return ref.at[1]
        return ref

    count = [0]

    def pass_on(o):
        for d in SPREAD.get(o, ()):
            label = o - d
            send(part(o, label), part(o, label), zs_sem.at[count[0]], zr_sem.at[label + 8],
                 (seq_at(d), t))
            count[0] += 1
        if abs(o) == 8:
            piece = part(8, o)
            send(piece, piece, ys_sem.at[o + 8], yr_sem.at[o + 8], across)
        else:
            send(buf.at[seq_at(o)], buf.at[seq_at(o)], ys_sem.at[o + 8], yr_sem.at[o + 8], across)

    pass_on(0)
    for label in LABELS:
        piece = part(label, label)
        copy_to(piece, piece, zs_sem.at[0], zr_sem.at[label + 8], across).wait_recv()
        pass_on(label)
    for label in (0,) + LABELS:
        ref = buf.at[seq_at(label, 1)]
        piece = ref.at[0] if label == -8 else ref.at[1] if label == 8 else ref
        copy_to(piece, piece, ys_sem.at[0], yr_sem.at[label + 8], across).wait_recv()
    xs[...] = buf[:, 0].astype(F32).reshape(xs.shape).astype(BF16)
    ys[...] = buf[:, 1].astype(F32).reshape(ys.shape).astype(BF16)
    for c in loads:
        c.wait()

    half = xs.shape[0] // 2
    mine = pl.ds(pl.multiple_of(core * half, half), half)
    theirs = pl.ds(pl.multiple_of((1 - core) * half, half), half)
    last = (((1,), (1,)), ((), ()))

    def product(k, at):
        rows_of, weight = ((xs, wg), (xs, wu), (ys, wd))[k]
        return lax.dot_general(rows_of[at, :], weight[...], last, preferred_element_type=F32)

    for k in range(3):
        far[k] = product(k, theirs)
        send(far.at[k], got.at[k], cs_sem.at[k], cr_sem.at[k], mate)
    for k in range(3):
        own[k] = product(k, mine)
    chips = slabs.shape[0]
    share = half // chips
    for k in range(3):
        copy_to(far.at[k], got.at[k], cs_sem.at[k], cr_sem.at[k], mate).wait_recv()
        total = own[k] + got[k]
        own[k] = total
        slabs[:, k] = total.reshape(chips, share, -1).astype(BF16)
    for i, k in enumerate(others):
        chip = chip_at(*k)
        send(slabs.at[chip], landed.at[i], ts_sem.at[i], tr_sem.at[i], (s, chip * 2 + core))
    me = chip_at(0, 0)
    sums = [own[k, pl.ds(pl.multiple_of(me * share, share), share), :] for k in range(3)]
    for i in range(len(others)):
        copy_to(slabs.at[0], landed.at[i], ts_sem.at[i], tr_sem.at[i], mate).wait_recv()
        for k in range(3):
            sums[k] = sums[k] + landed[i, k].astype(F32)
    gate, up, grad = sums
    sig = jax.nn.sigmoid(gate)
    silu = gate * sig
    at = core * chips + me
    act[at, 0] = (silu * up).astype(BF16)
    act[at, 1] = (grad * gate * sig).astype(BF16)
    act[at, 2] = (grad * up * sig * (1.0 + gate * (1.0 - sig))).astype(BF16)

    for i, k in enumerate(others):
        send(act.at[at], act.at[at], as_sem.at[i], ar_sem.at[i], (s, chip_at(*k) * 2 + core))
    send(act.at[at], act.at[at], bs_sem.at[7], br_sem.at[7], mate)
    for i, (a, b) in enumerate(others):
        from_chip = core * chips + chip_at(-a, b)
        ref = act.at[from_chip]
        copy_to(ref, ref, as_sem.at[i], ar_sem.at[i], mate).wait_recv()
        send(ref, ref, bs_sem.at[i], br_sem.at[i], mate)
    for i, (a, b) in list(enumerate(others)) + [(7, (0, 0))]:
        ref = act.at[(1 - core) * chips + chip_at(-a, b)]
        copy_to(ref, ref, bs_sem.at[i], br_sem.at[i], mate).wait_recv()

    tokens, units = xs.shape[0], wg.shape[0]
    gate_unit = act[:, 2].reshape(tokens, units)
    up_unit = act[:, 1].reshape(tokens, units)
    term = jnp.dot(gate_unit, wg[...], preferred_element_type=F32)
    term = term + jnp.dot(up_unit, wu[...], preferred_element_type=F32)
    dxp[...] = term.reshape(dxp.shape)

    for i, o in enumerate(Y_ORDER):
        ysend[i] = dxp[seq_at(-o, 1)].astype(BF16)
        send(ysend.at[i], yrecv.at[i], fys_sem.at[i], fyr_sem.at[i], across)

    first = (((0,), (0,)), ((), ()))
    gg[...] = lax.dot_general(gate_unit, xs[...], first, preferred_element_type=F32)
    ug[...] = lax.dot_general(up_unit, xs[...], first, preferred_element_type=F32)
    stores = [pltpu.make_async_copy(gg, gg_any, store_sem.at[0]),
              pltpu.make_async_copy(ug, ug_any, store_sem.at[1])]
    for c in stores:
        c.start()

    def column_term(o):
        i = Y_ORDER.index(8 if o == -8 else o)
        return dxp[seq_at(-o)] + yrecv[i].astype(F32)

    waited = set()

    def wait_y(o):
        i = Y_ORDER.index(8 if o == -8 else o)
        if i not in waited:
            waited.add(i)
            copy_to(ysend.at[i], yrecv.at[i], fys_sem.at[i], fyr_sem.at[i], across).wait_recv()

    wide = depth // 2

    def piece_of(ref, o):
        if o == 8:
            return ref.at[16, :, pl.ds(0, wide)]
        if o == -8:
            return ref.at[17, :, pl.ds(0, wide)]
        return ref.at[o + 8]

    def give(o, value):
        if o == 8:
            zsend[16, :, :wide] = value[:, :wide]
        elif o == -8:
            zsend[17, :, :wide] = value[:, wide:]
        else:
            zsend[o + 8] = value
        send(piece_of(zsend, o), piece_of(zrecv, o), fzs_sem.at[o + 8], fzr_sem.at[o + 8],
             (seq_at(PARENT[o] - o), t))

    def collected(o):
        wait_y(o)
        value = column_term(o)
        for c in CHILDREN[o]:
            ref = piece_of(zrecv, c)
            copy_to(ref, ref, fzs_sem.at[0], fzr_sem.at[c + 8], across).wait_recv()
        for c in CHILDREN[o]:
            if c == 8:
                value = value + jnp.concatenate(
                    [zrecv[16, :, :wide], jnp.zeros((rows, wide), F32)], axis=1)
            elif c == -8:
                value = value + jnp.concatenate(
                    [jnp.zeros((rows, wide), F32), zrecv[17, :, :wide]], axis=1)
            else:
                value = value + zrecv[c + 8]
        return value

    for o in LEAVES:
        wait_y(o)
        give(o, column_term(o))
    dg[...] = lax.dot_general(act[:, 0].reshape(tokens, units), ys[...], first,
                              preferred_element_type=F32)
    c = pltpu.make_async_copy(dg, dg_any, store_sem.at[2])
    c.start()
    stores.append(c)
    for o in (6, -6, 3, -3):
        give(o, collected(o))
    dx_ref[...] = collected(0).astype(BF16)

    for c in sent:
        c.wait_send()
    for c in stores:
        c.wait()


def solution(mesh):
    nz = mesh.shape["seq"] // 2
    nx = mesh.shape["tp"] // 4
    chips = mesh.shape["tp"] // 2

    def per_device(inputs, out_grad, gate_weight, up_weight, down_weight):
        groups, local, depth = inputs.shape
        rows = groups * local
        units = gate_weight.shape[1]
        tokens = rows * mesh.shape["seq"]
        half, share = tokens // 2, tokens // (2 * chips)
        whole = pl.BlockSpec(memory_space=pltpu.VMEM)
        anywhere = pl.BlockSpec(memory_space=pl.ANY)
        dma = pltpu.SemaphoreType.DMA
        vmem = pltpu.VMEM
        out = pl.pallas_call(
            lambda *refs: kernel(nz, nx, *refs),
            out_shape=(
                jax.ShapeDtypeStruct((rows, depth), BF16),
                jax.ShapeDtypeStruct((units, depth), F32),
                jax.ShapeDtypeStruct((units, depth), F32),
                jax.ShapeDtypeStruct((units, depth), F32),
            ),
            in_specs=[whole, whole, anywhere, anywhere, anywhere],
            out_specs=(whole, anywhere, anywhere, anywhere),
            scratch_shapes=[
                vmem((2 * nz, 2, rows, depth), BF16),
                vmem((units, depth), BF16), vmem((units, depth), BF16), vmem((units, depth), BF16),
                vmem((tokens, depth), BF16), vmem((tokens, depth), BF16),
                vmem((3, half, units), F32), vmem((3, half, units), F32),
                vmem((3, half, units), F32),
                vmem((chips, 3, share, units), BF16),
                vmem((chips - 1, 3, share, units), BF16),
                vmem((2 * chips, 3, share, units), BF16),
                vmem((2 * nz, rows, depth), F32),
                vmem((nz, rows, depth), BF16), vmem((nz, rows, depth), BF16),
                vmem((18, rows, depth), F32), vmem((18, rows, depth), F32),
                vmem((units, depth), F32), vmem((units, depth), F32), vmem((units, depth), F32),
                dma((3,)), dma((3,)),
                dma((16,)), dma((17,)), dma((17,)), dma((17,)),
                dma((3,)), dma((3,)),
                dma((7,)), dma((7,)), dma((7,)), dma((7,)), dma((8,)), dma((8,)),
                dma((16,)), dma((16,)), dma((17,)), dma((17,)),
            ],
            compiler_params=pltpu.CompilerParams(
                collective_id=0, has_side_effects=True, vmem_limit_bytes=48 * 2**20),
        )(inputs, out_grad, gate_weight.T, up_weight.T, down_weight)
        return out[0].reshape(groups, local, depth), out[1].T, out[2].T, out[3]

    return jax.shard_map(
        per_device, mesh=mesh,
        in_specs=(P(None, "seq", "tp"), P(None, "seq", "tp"), P("tp", "seq"), P("tp", "seq"),
                  P("seq", "tp")),
        out_specs=(P(None, "seq", "tp"), P("tp", "seq"), P("tp", "seq"), P("seq", "tp")),
        check_vma=False)
```

time: 243 us -> 72.7 us (0.30)
  waiting for transfers between devices: 108 us -> 0 us
  Pallas kernels: 0 us -> 63.9 us
  starting transfers between devices: 56.4 us -> 0 us
  blocking collectives: 48.2 us -> 0 us
  matrix products: 9.02 us -> 0 us
  local copies, waits for them, and re-layouts: 13.3 us -> 7.86 us
  other arithmetic: 4.74 us -> 0 us
    all_to_all x9 -> x0, waiting for transfers between devices: 108 us -> none  [the longest x5 51.3 us: sum_at_owner(): lax.all_to_all(blocks, axis, split_axis=0, concat_axis=0, tiled=True)]
    pallas_call x0 -> x1, Pallas kernels: none -> 63.9 us  [per_device(): pl.pallas_call(lambda *refs: kernel(nz, nx, *refs), out_shape=(jax.ShapeD...]
    all_to_all x9 -> x0, starting transfers between devices: 56.4 us -> none  [the longest x5 28.4 us: sum_at_owner(): lax.all_to_all(blocks, axis, split_axis=0, concat_axis=0, tiled=True)]
    all_gather x2 -> x0, blocking collectives: 43 us -> none  [in_one_piece(): result = lax.all_gather(both, axis, axis=dim, tiled=True)]
    dot_general x16 -> x0, matrix products: 9.02 us -> none  [the longest x2 1.98 us: per_device(): lax.dot_general(whole_grad, down_weight, contract_last, preferred_element...]
    all_to_all x1 -> x0, blocking collectives: 5.26 us -> none  [from_everyone(): lax.all_to_all(jnp.broadcast_to(value[None], (count, *value.shape)), axis...]
    unnamed x31 -> x13, local copies, waits for them, and re-layouts: 2.05 us -> 7.26 us
    reduce_sum x6 -> x0, other arithmetic: 3.44 us -> none  [the longest x5 3.1 us: sum_at_owner(): return arrived.sum(axis=0)]
  transfers between devices with their start and end apart: 9 -> 0, of which waited for: 9 -> 0; matrix products, arithmetic and copies ran while one was open for 5% -> 0% of each run, Pallas kernels for 0% -> 0%
where the time goes in v1:
time: 72.7 us; the launch traced here: 72.4 us
  Pallas kernels  63.9 us (88%)
  local copies, waits for them, and re-layouts  7.86 us (11%)
    pallas_call x1, Pallas kernels, per_device(): pl.pallas_call(lambda *refs: kernel(nz, nx, *refs), out_shape=(jax.ShapeD...  63.9 us
    unnamed x13, local copies, waits for them, and re-layouts  7.26 us

profile of v1, /device:TPU:1, one launch (start us, length us, event | category | flops | bytes accessed | tf_op | source)
XLA Modules:
  0.0 72.4 jit_solution(13926635362380141741)
XLA Ops:
  0.6 0.0 copy-start
  0.6 1.0 %copy-done = bf16[512,464]{0,1:T(8,128)(2,1)S(1)} copy-done((bf16[512,464]{0,1:T(8,128)(2,1)S(1)}, bf16[512,464]{0,1:T(8,128)(2,1)}, u32[]{:S(2)}) %copy-start) | copy-done | bytes 475160
  1.7 0.0 copy-start.1
  1.7 1.0 %copy-done.1 = bf16[512,464]{0,1:T(8,128)(2,1)S(1)} copy-done((bf16[512,464]{0,1:T(8,128)(2,1)S(1)}, bf16[512,464]{0,1:T(8,128)(2,1)}, u32[]{:S(2)}) %copy-start.1) | copy-done | bytes 475160
  2.7 0.0 copy-start.2
  2.7 1.0 %copy-done.2 = bf16[464,512]{1,0:T(8,128)(2,1)S(1)} copy-done((bf16[464,512]{1,0:T(8,128)(2,1)S(1)}, bf16[464,512]{1,0:T(8,128)(2,1)}, u32[]{:S(2)}) %copy-start.2) | copy-done | bytes 475160
  3.7 0.0 copy-start.3
  3.7 0.7 copy-done.3
  4.4 0.0 copy-start.4
  4.4 0.7 copy-done.4
  5.1 63.9 %shard_map.84 = (bf16[8,512]{1,0:T(8,128)(2,1)S(1)}, f32[464,512]{1,0:T(8,128)S(1)}, f32[464,512]{1,0:T(8,128)S(1)}, f32[464,512]{1,0:T(8,128)S(1)}) custom-call(bf16[2,4,512]{2,1,0:T(4,128)(2,1)S(1)} %copy-done.3, bf16[2,4,512]{2,1,0:T(4,128)(2,1)S(1)} %copy-done.4, bf16[464,512]{1,0:T(8,128)(2,1)S(1)} %bitcast.6, bf16[464,512]{1,0:T(8,128)(2,1)S(1)} %bitcast.7, ...), custom_call_target="tpu_custom_call" | custom-call | tf_op jit(solution)/shard_map/pallas_call | solution.py:252
  69.0 0.6 reshape.11
  69.6 0.9 %copy.12 = f32[512,464]{0,1:T(8,128)} copy(f32[512,464]{0,1:T(8,128)S(1)} %bitcast.5) | data formatting | bytes 1900544
  70.5 0.9 %copy.13 = f32[512,464]{0,1:T(8,128)} copy(f32[512,464]{0,1:T(8,128)S(1)} %bitcast.4) | data formatting | bytes 1900544
  71.4 0.9 %copy.14 = f32[464,512]{1,0:T(8,128)} copy(f32[464,512]{1,0:T(8,128)S(1)} %get-tuple-element.19) | data formatting | bytes 1900544
Async XLA Ops:
  0.6 1.0 %copy-start = (bf16[512,464]{0,1:T(8,128)(2,1)S(1)}, bf16[512,464]{0,1:T(8,128)(2,1)}, u32[]{:S(2)}) copy-start(bf16[512,464]{0,1:T(8,128)(2,1)} %param.7) | copy-start | bytes 1425412
  1.7 1.0 %copy-start.1 = (bf16[512,464]{0,1:T(8,128)(2,1)S(1)}, bf16[512,464]{0,1:T(8,128)(2,1)}, u32[]{:S(2)}) copy-start(bf16[512,464]{0,1:T(8,128)(2,1)} %param.8) | copy-start | bytes 1425412
  2.7 1.0 %copy-start.2 = (bf16[464,512]{1,0:T(8,128)(2,1)S(1)}, bf16[464,512]{1,0:T(8,128)(2,1)}, u32[]{:S(2)}) copy-start(bf16[464,512]{1,0:T(8,128)(2,1)} %refs_4_.1) | copy-start | bytes 1425412
  3.7 0.7 copy-start.3
  4.4 0.7 copy-start.4

commit v2 on v1

v2 whole, which is shorter than its diff:
```python
import functools

import jax
import jax.numpy as jnp
from jax import lax
from jax.experimental import pallas as pl
from jax.experimental.pallas import tpu as pltpu
from jax.sharding import PartitionSpec as P

MESH = pl.DeviceIdType.MESH
F32, BF16 = jnp.float32, jnp.bfloat16

FAR_Y = (0, 1, "M")


def onward(core, oz):
    far = "M" if core else "R"
    here = () if core else ((0, 0, "M"),)
    sign = 1 if oz > 0 else -1
    near = ((1, 0, "M"), (-1, 0, "M"))
    if oz == 0:
        return ((3, 0, far), (-3, 0, far)) + near + (FAR_Y,)
    if abs(oz) == 3:
        return ((3 * sign, 0, far),) + near + here + (FAR_Y,)
    if abs(oz) == 6:
        return ((2 * sign, 1, "M"), (2 * sign, 0, "M"), (1, 1, "M"), (-1, 1, "M")) + near + here + (FAR_Y,)
    return (FAR_Y,) if abs(oz) in (1, 2, 4) else ()


def carrier(core, oz):
    return 1 if core or abs(oz) in (3, 6) else 0


INNER = (0, 1, -1, 3, -3, 2, -2, 4, -4, 6, -6)
EDGES = [(core, oz, dz, dy, kind) for core in (1, 0) for oz in INNER for dz, dy, kind in onward(core, oz)]
UP = {(core, oz + dz, dy, kind): (oz, dz, dy) for core, oz, dz, dy, kind in EDGES}


def is_inner(core, oz, dy, kind):
    return dy == 0 and oz in INNER and (kind == "R" or carrier(core, oz) == core)


LEAF_KEYS = [k for k in UP if not is_inner(*k)]
INNER_KEYS = [k for k in UP if is_inner(*k)]
HELD = [k for k in dict.fromkeys((oz + dz, dy) for _, oz, dz, dy, kind in EDGES if kind == "M")]
RELAYED = [3, -3, 6, -6]


def kernel(nz, nx, x_any, dy_any, wg_any, wu_any, wd_any, dx_ref, gg, ug, dg,
           xin, dyin, buf, relay, wg, wu, wd, xs, ys, own, far, got, slabs, landed, act,
           dxp, leaves, lrecv, zsend, zrecv,
           load_sem, zs_sem, zr_sem, rr_sem, cs_sem, cr_sem,
           ts_sem, tr_sem, as_sem, ar_sem, bs_sem, br_sem, fys_sem, fyr_sem, fzs_sem, fzr_sem):
    s = lax.axis_index("seq")
    t = lax.axis_index("tp")
    z, yl = s // 2, s % 2
    core, yh, x = t % 2, (t // 2) % 2, t // 4

    along = {(d, f): lax.rem(z + d + nz, nz) * 2 + (1 - yl if f else yl) for d in range(-8, 9) for f in (0, 1)}
    def seq_at(dz, flip=0):
        return along[dz, flip]

    def chip_at(dx, dyh):
        return lax.rem(x + dx + nx, nx) * 2 + lax.rem(yh + dyh, 2)

    others = [(2, 1), (1, 1), (3, 1), (2, 0), (0, 1), (1, 0), (3, 0)]

    def copy_to(src, dst, send, recv, device):
        return pltpu.make_async_remote_copy(
            src_ref=src, dst_ref=dst, send_sem=send, recv_sem=recv, device_id=device,
            device_id_type=MESH)

    mate = (s, t + 1 - 2 * core)
    across = (seq_at(0, 1), t)
    barrier = pltpu.get_barrier_semaphore()
    on_core = (t - core, t - core + 1)

    def met_by(c):
        met = {(0, 0, 1 - c)}
        for owner, oz, dz, dy, kind in EDGES:
            a, b = carrier(owner, oz), 1 if kind == "R" else owner
            met |= {(dz, dy, b)} if a == c else set()
            met |= {(-dz, dy, a)} if b == c else set()
        return sorted(met - {(0, 0, c)}, key=lambda m: (-abs(m[0]), m))

    def greet(c):
        partners = [(along[d, f], on_core[k]) for d, f, k in met_by(c)]
        partners += [(s, chip * 2 + core) for chip in chips_at]
        for device in partners:
            pl.semaphore_signal(barrier, inc=1, device_id=device, device_id_type=MESH)

    def greeted(c):
        pl.semaphore_wait(barrier, len(met_by(c)) + len(others))

    def on_cores(body):
        for c in (1, 0):
            pl.when(core == c)(functools.partial(body, c))

    chips_at = [chip_at(*k) for k in others]
    loads = [pltpu.make_async_copy(a, b, load_sem.at[i])
             for i, (a, b) in enumerate(((x_any, xin), (dy_any, dyin), (wg_any, wg), (wu_any, wu), (wd_any, wd)))]
    for c in loads[:2]:
        c.start()
    on_cores(greet)
    rows, depth = buf.shape[2], buf.shape[3]
    for c in loads[:2]:
        c.wait()
    buf[s, 0] = xin[...].reshape(rows, depth)
    buf[s, 1] = dyin[...].reshape(rows, depth)
    for c in loads[2:]:
        c.start()
    on_cores(greeted)

    sent = []

    def done():
        for c in sent:
            c.wait_send()
        for k in (0, 1):
            @pl.when(core == k)
            def _(k=k):
                for make in later[k]:
                    make().wait_send()

    def send(*a):
        c = copy_to(*a)
        c.start()
        sent.append(c)

    later = {0: [], 1: []}

    def tp_of(c):
        return on_core[c]

    def issue(c, make):
        make().start()
        later[c].append(make)

    def half_of(ref, oz):
        return ref.at[0] if oz == 8 else ref.at[1] if oz == -8 else ref

    def held(oz, dy):
        return half_of(buf.at[seq_at(-oz, dy)], oz)

    def pass_on(c, oz, kind, by):
        for dz, dy, to in onward(c, oz):
            n = EDGES.index((c, oz, dz, dy, to))
            far = oz + dz

            def make(dz=dz, dy=dy, to=to, n=n, far=far):
                src = relay.at[RELAYED.index(oz)] if kind == "R" else buf.at[seq_at(-oz)]
                dst = relay.at[RELAYED.index(far)] if to == "R" else buf.at[seq_at(-oz)]
                sem = rr_sem.at[RELAYED.index(far)] if to == "R" else zr_sem.at[HELD.index((far, dy))]
                return copy_to(half_of(src, far), half_of(dst, far), zs_sem.at[n], sem,
                               (seq_at(dz, dy), tp_of(1 if to == "R" else c)))
            issue(by, make)

    def arrived(oz, dy):
        ref = held(oz, dy)
        copy_to(ref, ref, zs_sem.at[0], zr_sem.at[HELD.index((oz, dy))], across).wait_recv()

    def relay_arrived(oz):
        i = RELAYED.index(oz)
        copy_to(relay.at[i], relay.at[i], zs_sem.at[0], rr_sem.at[i], across).wait_recv()

    @pl.when(core == 1)
    def _():
        pass_on(1, 0, "M", 1)
        for oz in (1, -1):
            arrived(oz, 0)
            pass_on(1, oz, "M", 1)
        for oz in (3, -3):
            arrived(oz, 0)
            pass_on(1, oz, "M", 1)
        for oz in (3, -3):
            relay_arrived(oz)
            pass_on(0, oz, "R", 1)
        for oz in (2, -2, 4, -4):
            arrived(oz, 0)
            pass_on(1, oz, "M", 1)
        for oz in (6, -6):
            arrived(oz, 0)
            pass_on(1, oz, "M", 1)
        for oz in (6, -6):
            relay_arrived(oz)
            pass_on(0, oz, "R", 1)
        for oz, dy in HELD:
            if dy or oz not in INNER:
                arrived(oz, dy)

    @pl.when(core == 0)
    def _():
        pass_on(0, 0, "M", 0)
        for oz in (1, -1, 2, -2, 4, -4):
            arrived(oz, 0)
            pass_on(0, oz, "M", 0)
        for oz, dy in HELD:
            if dy or oz not in (0, 1, -1, 2, -2, 4, -4):
                arrived(oz, dy)

    xs[...] = buf[:, 0].astype(F32).reshape(xs.shape).astype(BF16)
    ys[...] = buf[:, 1].astype(F32).reshape(ys.shape).astype(BF16)
    for c in loads[2:]:
        c.wait()

    half = xs.shape[0] // 2
    mine = pl.ds(pl.multiple_of(core * half, half), half)
    theirs = pl.ds(pl.multiple_of((1 - core) * half, half), half)
    last = (((1,), (1,)), ((), ()))

    def product(k, at):
        rows_of, weight = ((xs, wg), (xs, wu), (ys, wd))[k]
        return lax.dot_general(rows_of[at, :], weight[...], last, preferred_element_type=F32)

    chips = slabs.shape[1]
    share = half // chips
    for k in range(3):
        far[k] = product(k, theirs)
        send(far.at[k], got.at[k], cs_sem.at[k], cr_sem.at[k], mate)
    own[0] = product(0, mine)
    for k in range(3):
        copy_to(far.at[k], got.at[k], cs_sem.at[k], cr_sem.at[k], mate).wait_recv()
        total = own[k] + got[k]
        own[k] = total
        slabs[k] = total.reshape(chips, share, -1).astype(BF16)
        for i, (a, b) in enumerate(others):
            chip = chip_at(a, b)
            send(slabs.at[k, chip], landed.at[i, k], ts_sem.at[i, k], tr_sem.at[i, k],
                 (s, chip * 2 + core))
        if k < 2:
            own[k + 1] = product(k + 1, mine)
    me = chip_at(0, 0)
    sums = [own[k, pl.ds(pl.multiple_of(me * share, share), share), :] for k in range(3)]
    for k in range(3):
        for i in range(len(others)):
            copy_to(slabs.at[k, 0], landed.at[i, k], ts_sem.at[i, k], tr_sem.at[i, k], mate).wait_recv()
            sums[k] = sums[k] + landed[i, k].astype(F32)
    gate, up, grad = sums
    sig = jax.nn.sigmoid(gate)
    silu = gate * sig
    at = core * chips + me
    act[at, 0] = (silu * up).astype(BF16)
    act[at, 1] = (grad * gate * sig).astype(BF16)
    act[at, 2] = (grad * up * sig * (1.0 + gate * (1.0 - sig))).astype(BF16)

    for i, k in enumerate(others):
        send(act.at[at], act.at[at], as_sem.at[i], ar_sem.at[i], (s, chip_at(*k) * 2 + core))
    send(act.at[at], act.at[at], bs_sem.at[7], br_sem.at[7], mate)
    for i, (a, b) in enumerate(others):
        from_chip = core * chips + chip_at(-a, b)
        ref = act.at[from_chip]
        copy_to(ref, ref, as_sem.at[i], ar_sem.at[i], mate).wait_recv()
        send(ref, ref, bs_sem.at[i], br_sem.at[i], mate)
    for i, (a, b) in list(enumerate(others)) + [(7, (0, 0))]:
        ref = act.at[(1 - core) * chips + chip_at(-a, b)]
        copy_to(ref, ref, bs_sem.at[i], br_sem.at[i], mate).wait_recv()

    tokens, units = xs.shape[0], wg.shape[0]
    gate_unit = act[:, 2].reshape(tokens, units)
    up_unit = act[:, 1].reshape(tokens, units)
    term = jnp.dot(gate_unit, wg[...], preferred_element_type=F32)
    term = term + jnp.dot(up_unit, wu[...], preferred_element_type=F32)
    dxp[...] = term.reshape(dxp.shape)

    leaves[...] = term.reshape(dxp.shape).astype(BF16)
    first = (((0,), (0,)), ((), ()))
    wide = depth // 2

    def side(ref, oz):
        return ref.at[:, pl.ds(0, wide)] if oz == 8 else ref.at[:, pl.ds(wide, wide)] if oz == -8 else ref

    def send_up(key, by):
        c, oz, dy, kind = key
        up, dz, _ = UP[key]
        target = (seq_at(-dz, dy), tp_of(carrier(c, up)))
        if key in INNER_KEYS:
            n = INNER_KEYS.index(key)
            issue(by, lambda: copy_to(zsend.at[n], zrecv.at[n], fzs_sem.at[n], fzr_sem.at[n], target))
        else:
            n = LEAF_KEYS.index(key)
            issue(by, lambda: copy_to(side(leaves.at[seq_at(-oz, dy)], oz), side(lrecv.at[n], oz),
                                      fys_sem.at[n], fyr_sem.at[n], target))

    def collected(c, oz):
        kind = "R" if carrier(c, oz) != c else "M"
        value = jnp.zeros((rows, depth), F32) if kind == "R" else dxp[seq_at(-oz)]
        for dz, dy, to in onward(c, oz):
            key = (c, oz + dz, dy, to)
            if key in INNER_KEYS:
                n = INNER_KEYS.index(key)
                copy_to(zsend.at[n], zrecv.at[n], fzs_sem.at[n], fzr_sem.at[n], across).wait_recv()
                value = value + zrecv[n]
            else:
                n = LEAF_KEYS.index(key)
                ref = side(lrecv.at[n], key[1])
                copy_to(ref, ref, fys_sem.at[n], fyr_sem.at[n], across).wait_recv()
                nothing = jnp.zeros((rows, wide), F32)
                if key[1] == 8:
                    value = value + jnp.concatenate([lrecv[n, :, :wide].astype(F32), nothing], axis=1)
                elif key[1] == -8:
                    value = value + jnp.concatenate([nothing, lrecv[n, :, wide:].astype(F32)], axis=1)
                else:
                    value = value + lrecv[n].astype(F32)
        return value

    def forward(c, oz, by):
        key = (c, oz, 0, "R" if carrier(c, oz) != c else "M")
        zsend[INNER_KEYS.index(key)] = collected(c, oz)
        send_up(key, by)

    urgent = (8, 7, 5, 6, 4, 2, 3, 1, 0)

    def start_leaves(c):
        mine = [k for k in LEAF_KEYS if k[0] == c]
        for key in sorted(mine, key=lambda k: (urgent.index(abs(k[1])), -k[2])):
            send_up(key, c)

    def middle(c):
        for oz in (4, -4, 2, -2, 1, -1):
            forward(c, oz, c)

    def outer(c):
        for oz in (6, -6):
            for b in ((1, 0) if c else ()):
                forward(b, oz, c)

    def finish(c):
        for oz in (3, -3):
            for b in ((1, 0) if c else ()):
                forward(b, oz, c)
        dx_ref[...] = collected(c, 0).astype(BF16)

    on_cores(start_leaves)
    gg[...] = lax.dot_general(gate_unit, xs[...], first, preferred_element_type=F32)
    on_cores(middle)
    on_cores(outer)
    ug[...] = lax.dot_general(up_unit, xs[...], first, preferred_element_type=F32)
    dg[...] = lax.dot_general(act[:, 0].reshape(tokens, units), ys[...], first,
                              preferred_element_type=F32)
    on_cores(finish)

    done()


def write_out(dx, gg, ug, dg, dx_out, gg_out, ug_out, dg_out, staged, sem):
    copies = [pltpu.make_async_copy(a, b, sem.at[i])
              for i, (a, b) in enumerate(((gg, gg_out), (ug, ug_out), (dg, dg_out)))]
    for c in copies:
        c.start()
    staged[...] = dx[...].reshape(staged.shape)
    copies.append(pltpu.make_async_copy(staged, dx_out, sem.at[3]))
    copies[3].start()
    for c in copies:
        c.wait()


def solution(mesh):
    nz = mesh.shape["seq"] // 2
    nx = mesh.shape["tp"] // 4
    chips = mesh.shape["tp"] // 2

    def per_device(inputs, out_grad, gate_weight, up_weight, down_weight):
        groups, local, depth = inputs.shape
        rows = groups * local
        units = gate_weight.shape[1]
        tokens = rows * mesh.shape["seq"]
        half, share = tokens // 2, tokens // (2 * chips)
        whole = pl.BlockSpec(memory_space=pltpu.VMEM)
        hbm = pl.BlockSpec(memory_space=pltpu.HBM)
        dma = pltpu.SemaphoreType.DMA
        vmem = pltpu.VMEM
        out = pl.pallas_call(
            lambda *refs: kernel(nz, nx, *refs),
            out_shape=(
                vmem((rows, depth), BF16),
                vmem((units, depth), F32), vmem((units, depth), F32), vmem((units, depth), F32),
            ),
            in_specs=[hbm] * 5,
            out_specs=(whole,) * 4,
            scratch_shapes=[
                vmem((groups, local, depth), BF16), vmem((groups, local, depth), BF16),
                vmem((2 * nz, 2, rows, depth), BF16), vmem((4, 2, rows, depth), BF16),
                vmem((units, depth), BF16), vmem((units, depth), BF16), vmem((units, depth), BF16),
                vmem((tokens, depth), BF16), vmem((tokens, depth), BF16),
                vmem((3, half, units), F32), vmem((3, half, units), F32),
                vmem((3, half, units), F32),
                vmem((3, chips, share, units), BF16),
                vmem((chips - 1, 3, share, units), BF16),
                vmem((2 * chips, 3, share, units), BF16),
                vmem((2 * nz, rows, depth), F32),
                vmem((2 * nz, rows, depth), BF16), vmem((len(LEAF_KEYS), rows, depth), BF16),
                vmem((len(INNER_KEYS), rows, depth), F32), vmem((len(INNER_KEYS), rows, depth), F32),
                dma((5,)),
                dma((len(EDGES),)), dma((len(HELD),)), dma((4,)),
                dma((3,)), dma((3,)),
                dma((7, 3)), dma((7, 3)), dma((7,)), dma((7,)), dma((8,)), dma((8,)),
                dma((len(LEAF_KEYS),)), dma((len(LEAF_KEYS),)),
                dma((len(INNER_KEYS),)), dma((len(INNER_KEYS),)),
            ],
            compiler_params=pltpu.CompilerParams(
                collective_id=0, has_side_effects=True, vmem_limit_bytes=48 * 2**20),
        )(*[pltpu.with_memory_space_constraint(a, pltpu.HBM) for a in (
            inputs, out_grad, gate_weight.T, up_weight.T, down_weight)])
        grad = jax.ShapeDtypeStruct((units, depth), F32)
        dx, gg, ug, dg = pl.pallas_call(
            write_out,
            out_shape=(jax.ShapeDtypeStruct((groups, local, depth), BF16), grad, grad, grad),
            in_specs=[whole] * 4,
            out_specs=(hbm,) * 4,
            scratch_shapes=[vmem((groups, local, depth), BF16), dma((4,))],
            compiler_params=pltpu.CompilerParams(vmem_limit_bytes=8 * 2**20),
        )(*out)
        return dx, gg.T, ug.T, dg

    return jax.shard_map(
        per_device, mesh=mesh,
        in_specs=(P(None, "seq", "tp"), P(None, "seq", "tp"), P("tp", "seq"), P("tp", "seq"),
                  P("seq", "tp")),
        out_specs=(P(None, "seq", "tp"), P("tp", "seq"), P("tp", "seq"), P("seq", "tp")),
        check_vma=False)
```

time: 72.7 us -> 62.8 us (0.86)
  local copies, waits for them, and re-layouts: 7.86 us -> 0 us
  Pallas kernels: 63.9 us -> 61.9 us
    unnamed x13 -> x0, local copies, waits for them, and re-layouts: 7.26 us -> none
    pallas_call x1 -> x2, Pallas kernels: 63.9 us -> 61.9 us  [the longest x1 60.3 us: per_device(): pl.pallas_call(lambda *refs: kernel(nz, nx, *refs), out_shape=(vmem((rows...]
where the time goes in v2:
time: 62.8 us; the launch traced here: 62.6 us
  Pallas kernels  61.9 us (99%)
  between operations  0.64 us (1%)
    pallas_call x1, Pallas kernels, per_device(): pl.pallas_call(lambda *refs: kernel(nz, nx, *refs), out_shape=(vmem((rows...  60.3 us
    pallas_call x1, Pallas kernels, per_device(): pl.pallas_call(write_out, out_shape=(jax.ShapeDtypeStruct((groups, local,...  1.6 us

profile of v2, /device:TPU:1, one launch (start us, length us, event | category | flops | bytes accessed | tf_op | source)
XLA Modules:
  0.0 62.6 jit_solution(8262325844359017569)
XLA Ops:
  0.6 60.3 %shard_map.84 = (bf16[8,512]{1,0:T(8,128)(2,1)S(1)}, f32[464,512]{1,0:T(8,128)S(1)}, f32[464,512]{1,0:T(8,128)S(1)}, f32[464,512]{1,0:T(8,128)S(1)}) custom-call(bf16[2,4,512]{2,1,0:T(4,128)(2,1)} %refs_0_.1, bf16[2,4,512]{2,1,0:T(4,128)(2,1)} %refs_1_.1, bf16[464,512]{1,0:T(8,128)(2,1)} %bitcast.4, bf16[464,512]{1,0:T(8,128)(2,1)} %bitcast.5, ...), custom_call_target="tpu_custom_call" | custom-call | tf_op jit(solution)/shard_map/pallas_call | solution.py:372
  61.0 1.6 %shard_map.85 = (bf16[2,4,512]{2,1,0:T(4,128)(2,1)}, f32[464,512]{1,0:T(8,128)}, f32[464,512]{1,0:T(8,128)}, f32[464,512]{1,0:T(8,128)}) custom-call(bf16[8,512]{1,0:T(8,128)(2,1)S(1)} %get-tuple-element.12.dx, f32[464,512]{1,0:T(8,128)S(1)} %get-tuple-element.13.gg, f32[464,512]{1,0:T(8,128)S(1)} %get-tuple-element.14.ug, f32[464,512]{1,0:T(8,128)S(1)} %get-tuple-element.15.dg), custom_call_target="tpu_custom_call" | custom-call | tf_op jit(solution)/shard_map/pallas_call | solution.py:405

commit v3 on v2

--- a/solution.py
+++ b/solution.py
@@ -33,7 +33,16 @@
 
 INNER = (0, 1, -1, 3, -3, 2, -2, 4, -4, 6, -6)
 EDGES = [(core, oz, dz, dy, kind) for core in (1, 0) for oz in INNER for dz, dy, kind in onward(core, oz)]
-UP = {(core, oz + dz, dy, kind): (oz, dz, dy) for core, oz, dz, dy, kind in EDGES}
+
+
+def inward(core, oz):
+    far = "M" if core else "R"
+    edges = tuple(e for e in onward(core, oz) if abs(oz) != 3 or abs(e[0]) != 3)
+    return edges + (((6, 0, far), (-6, 0, far)) if oz == 0 else ())
+
+
+UP = {(core, oz + dz, dy, kind): (oz, dz, dy)
+      for core in (1, 0) for oz in INNER for dz, dy, kind in inward(core, oz)}
 
 
 def is_inner(core, oz, dy, kind):
@@ -49,7 +58,7 @@
 def kernel(nz, nx, x_any, dy_any, wg_any, wu_any, wd_any, dx_ref, gg, ug, dg,
            xin, dyin, buf, relay, wg, wu, wd, xs, ys, own, far, got, slabs, landed, act,
            dxp, leaves, lrecv, zsend, zrecv,
-           load_sem, zs_sem, zr_sem, rr_sem, cs_sem, cr_sem,
+           ready, load_sem, zs_sem, zr_sem, rr_sem, cs_sem, cr_sem,
            ts_sem, tr_sem, as_sem, ar_sem, bs_sem, br_sem, fys_sem, fyr_sem, fzs_sem, fzr_sem):
     s = lax.axis_index("seq")
     t = lax.axis_index("tp")
@@ -85,18 +94,24 @@
 
     def greet(c):
         partners = [(along[d, f], on_core[k]) for d, f, k in met_by(c)]
-        partners += [(s, chip * 2 + core) for chip in chips_at]
+        partners += [(s, chips_at[others.index(k)] * 2 + core) for k in close]
         for device in partners:
             pl.semaphore_signal(barrier, inc=1, device_id=device, device_id_type=MESH)
 
     def greeted(c):
-        pl.semaphore_wait(barrier, len(met_by(c)) + len(others))
+        pl.semaphore_wait(barrier, len(met_by(c)) + len(close))
+        for device in [(s, chips_at[others.index((0, 1))] * 2 + core)] + [(along[d, 0], t) for d in (3, -3) if c]:
+            pl.semaphore_signal(ready, inc=1, device_id=device, device_id_type=MESH)
+
+    def all_ready(c):
+        pl.semaphore_wait(ready, 3 if c else 1)
 
     def on_cores(body):
         for c in (1, 0):
             pl.when(core == c)(functools.partial(body, c))
 
     chips_at = [chip_at(*k) for k in others]
+    close = [(2, 0), (0, 1), (1, 0), (3, 0)]
     loads = [pltpu.make_async_copy(a, b, load_sem.at[i])
              for i, (a, b) in enumerate(((x_any, xin), (dy_any, dyin), (wg_any, wg), (wu_any, wu), (wd_any, wd)))]
     for c in loads[:2]:
@@ -214,6 +229,7 @@
 
     chips = slabs.shape[1]
     share = half // chips
+    on_cores(all_ready)
     for k in range(3):
         far[k] = product(k, theirs)
         send(far.at[k], got.at[k], cs_sem.at[k], cr_sem.at[k], mate)
@@ -230,30 +246,48 @@
         if k < 2:
             own[k + 1] = product(k + 1, mine)
     me = chip_at(0, 0)
-    sums = [own[k, pl.ds(pl.multiple_of(me * share, share), share), :] for k in range(3)]
+    at = core * chips + me
+    sums = []
     for k in range(3):
+        total = own[k, pl.ds(pl.multiple_of(me * share, share), share), :]
         for i in range(len(others)):
             copy_to(slabs.at[k, 0], landed.at[i, k], ts_sem.at[i, k], tr_sem.at[i, k], mate).wait_recv()
-            sums[k] = sums[k] + landed[i, k].astype(F32)
-    gate, up, grad = sums
-    sig = jax.nn.sigmoid(gate)
-    silu = gate * sig
-    at = core * chips + me
-    act[at, 0] = (silu * up).astype(BF16)
+            total = total + landed[i, k].astype(F32)
+        sums.append(total)
+        if k == 1:
+            gate, up = sums
+            sig = jax.nn.sigmoid(gate)
+            act[at, 0] = (gate * sig * up).astype(BF16)
+    grad = sums[2]
     act[at, 1] = (grad * gate * sig).astype(BF16)
     act[at, 2] = (grad * up * sig * (1.0 + gate * (1.0 - sig))).astype(BF16)
 
-    for i, k in enumerate(others):
-        send(act.at[at], act.at[at], as_sem.at[i], ar_sem.at[i], (s, chip_at(*k) * 2 + core))
-    send(act.at[at], act.at[at], bs_sem.at[7], br_sem.at[7], mate)
-    for i, (a, b) in enumerate(others):
-        from_chip = core * chips + chip_at(-a, b)
-        ref = act.at[from_chip]
-        copy_to(ref, ref, as_sem.at[i], ar_sem.at[i], mate).wait_recv()
-        send(ref, ref, bs_sem.at[i], br_sem.at[i], mate)
-    for i, (a, b) in list(enumerate(others)) + [(7, (0, 0))]:
-        ref = act.at[(1 - core) * chips + chip_at(-a, b)]
-        copy_to(ref, ref, bs_sem.at[i], br_sem.at[i], mate).wait_recv()
+    def units_of(g, late):
+        return act.at[g, 0] if late else act.at[g, pl.ds(1, 2)]
+
+    def give_units(late):
+        ref = units_of(at, late)
+        for i, chip in enumerate(chips_at):
+            send(ref, ref, as_sem.at[i, late], ar_sem.at[i, late], (s, chip * 2 + core))
+        send(ref, ref, bs_sem.at[7, late], br_sem.at[7, late], mate)
+
+    from_chips = [chip_at(-a, b) for a, b in others] + [me]
+
+    def hand_over_units(late):
+        for i in range(len(others)):
+            ref = units_of(core * chips + from_chips[i], late)
+            copy_to(ref, ref, as_sem.at[i, late], ar_sem.at[i, late], mate).wait_recv()
+            send(ref, ref, bs_sem.at[i, late], br_sem.at[i, late], mate)
+
+    def units_complete(late):
+        for i, chip in enumerate(from_chips):
+            ref = units_of((1 - core) * chips + chip, late)
+            copy_to(ref, ref, bs_sem.at[i, late], br_sem.at[i, late], mate).wait_recv()
+
+    give_units(0)
+    give_units(1)
+    hand_over_units(0)
+    units_complete(0)
 
     tokens, units = xs.shape[0], wg.shape[0]
     gate_unit = act[:, 2].reshape(tokens, units)
@@ -284,7 +318,7 @@
     def collected(c, oz):
         kind = "R" if carrier(c, oz) != c else "M"
         value = jnp.zeros((rows, depth), F32) if kind == "R" else dxp[seq_at(-oz)]
-        for dz, dy, to in onward(c, oz):
+        for dz, dy, to in inward(c, oz):
             key = (c, oz + dz, dy, to)
             if key in INNER_KEYS:
                 n = INNER_KEYS.index(key)
@@ -331,10 +365,12 @@
         dx_ref[...] = collected(c, 0).astype(BF16)
 
     on_cores(start_leaves)
+    hand_over_units(1)
     gg[...] = lax.dot_general(gate_unit, xs[...], first, preferred_element_type=F32)
     on_cores(middle)
     on_cores(outer)
     ug[...] = lax.dot_general(up_unit, xs[...], first, preferred_element_type=F32)
+    units_complete(1)
     dg[...] = lax.dot_general(act[:, 0].reshape(tokens, units), ys[...], first,
                               preferred_element_type=F32)
     on_cores(finish)
@@ -390,10 +426,10 @@
                 vmem((2 * nz, rows, depth), F32),
                 vmem((2 * nz, rows, depth), BF16), vmem((len(LEAF_KEYS), rows, depth), BF16),
                 vmem((len(INNER_KEYS), rows, depth), F32), vmem((len(INNER_KEYS), rows, depth), F32),
-                dma((5,)),
+                pltpu.SemaphoreType.REGULAR, dma((5,)),
                 dma((len(EDGES),)), dma((len(HELD),)), dma((4,)),
                 dma((3,)), dma((3,)),
-                dma((7, 3)), dma((7, 3)), dma((7,)), dma((7,)), dma((8,)), dma((8,)),
+                dma((7, 3)), dma((7, 3)), dma((7, 2)), dma((7, 2)), dma((8, 2)), dma((8, 2)),
                 dma((len(LEAF_KEYS),)), dma((len(LEAF_KEYS),)),
                 dma((len(INNER_KEYS),)), dma((len(INNER_KEYS),)),
             ],

time: 62.8 us -> 60.1 us (0.957)
  Pallas kernels: 61.9 us -> 59.2 us
    pallas_call x1, Pallas kernels: 60.3 us -> 57.6 us  [per_device(): pl.pallas_call(lambda *refs: kernel(nz, nx, *refs), out_shape=(vmem((rows...]
where the time goes in v3:
time: 60.1 us; the launch traced here: 59.9 us
  Pallas kernels  59.2 us (99%)
  between operations  0.64 us (1%)
    pallas_call x1, Pallas kernels, per_device(): pl.pallas_call(lambda *refs: kernel(nz, nx, *refs), out_shape=(vmem((rows...  57.6 us
    pallas_call x1, Pallas kernels, per_device(): pl.pallas_call(write_out, out_shape=(jax.ShapeDtypeStruct((groups, local,...  1.6 us

profile of v3, /device:TPU:1, one launch (start us, length us, event | category | flops | bytes accessed | tf_op | source)
XLA Modules:
  0.0 59.9 jit_solution(9445225308982421769)
XLA Ops:
  0.6 57.6 %shard_map.84 = (bf16[8,512]{1,0:T(8,128)(2,1)S(1)}, f32[464,512]{1,0:T(8,128)S(1)}, f32[464,512]{1,0:T(8,128)S(1)}, f32[464,512]{1,0:T(8,128)S(1)}) custom-call(bf16[2,4,512]{2,1,0:T(4,128)(2,1)} %refs_0_.1, bf16[2,4,512]{2,1,0:T(4,128)(2,1)} %refs_1_.1, bf16[464,512]{1,0:T(8,128)(2,1)} %bitcast.4, bf16[464,512]{1,0:T(8,128)(2,1)} %bitcast.5, ...), custom_call_target="tpu_custom_call" | custom-call | tf_op jit(solution)/shard_map/pallas_call | solution.py:408
  58.3 1.6 %shard_map.85 = (bf16[2,4,512]{2,1,0:T(4,128)(2,1)}, f32[464,512]{1,0:T(8,128)}, f32[464,512]{1,0:T(8,128)}, f32[464,512]{1,0:T(8,128)}) custom-call(bf16[8,512]{1,0:T(8,128)(2,1)S(1)} %get-tuple-element.12.dx, f32[464,512]{1,0:T(8,128)S(1)} %get-tuple-element.13.gg, f32[464,512]{1,0:T(8,128)S(1)} %get-tuple-element.14.ug, f32[464,512]{1,0:T(8,128)S(1)} %get-tuple-element.15.dg), custom_call_target="tpu_custom_call" | custom-call | tf_op jit(solution)/shard_map/pallas_call | solution.py:441

commit v4 on v3

--- a/solution.py
+++ b/solution.py
@@ -131,11 +131,13 @@
     def done():
         for c in sent:
             c.wait_send()
-        for k in (0, 1):
-            @pl.when(core == k)
-            def _(k=k):
-                for make in later[k]:
-                    make().wait_send()
+        sent.clear()
+
+        def left(c):
+            for make in later[c]:
+                make().wait_send()
+            later[c].clear()
+        on_cores(left)
 
     def send(*a):
         c = copy_to(*a)
@@ -151,72 +153,65 @@
         make().start()
         later[c].append(make)
 
-    def half_of(ref, oz):
-        return ref.at[0] if oz == 8 else ref.at[1] if oz == -8 else ref
-
-    def held(oz, dy):
-        return half_of(buf.at[seq_at(-oz, dy)], oz)
-
-    def pass_on(c, oz, kind, by):
+    wide = depth // 2
+
+    def side(ref, oz):
+        return ref.at[:, pl.ds(0, wide)] if oz == 8 else ref.at[:, pl.ds(wide, wide)] if oz == -8 else ref
+
+    def pass_on(c, oz, j, by):
+        relays = carrier(c, oz) != c
         for dz, dy, to in onward(c, oz):
             n = EDGES.index((c, oz, dz, dy, to))
             far = oz + dz
 
             def make(dz=dz, dy=dy, to=to, n=n, far=far):
-                src = relay.at[RELAYED.index(oz)] if kind == "R" else buf.at[seq_at(-oz)]
-                dst = relay.at[RELAYED.index(far)] if to == "R" else buf.at[seq_at(-oz)]
-                sem = rr_sem.at[RELAYED.index(far)] if to == "R" else zr_sem.at[HELD.index((far, dy))]
-                return copy_to(half_of(src, far), half_of(dst, far), zs_sem.at[n], sem,
+                src = relay.at[RELAYED.index(oz), j] if relays else buf.at[seq_at(-oz), j]
+                dst = relay.at[RELAYED.index(far), j] if to == "R" else buf.at[seq_at(-oz), j]
+                sem = rr_sem.at[RELAYED.index(far), j] if to == "R" else zr_sem.at[HELD.index((far, dy)), j]
+                return copy_to(side(src, far), side(dst, far), zs_sem.at[n, j], sem,
                                (seq_at(dz, dy), tp_of(1 if to == "R" else c)))
             issue(by, make)
 
-    def arrived(oz, dy):
-        ref = held(oz, dy)
-        copy_to(ref, ref, zs_sem.at[0], zr_sem.at[HELD.index((oz, dy))], across).wait_recv()
-
-    def relay_arrived(oz):
-        i = RELAYED.index(oz)
-        copy_to(relay.at[i], relay.at[i], zs_sem.at[0], rr_sem.at[i], across).wait_recv()
-
-    @pl.when(core == 1)
-    def _():
-        pass_on(1, 0, "M", 1)
-        for oz in (1, -1):
-            arrived(oz, 0)
-            pass_on(1, oz, "M", 1)
-        for oz in (3, -3):
-            arrived(oz, 0)
-            pass_on(1, oz, "M", 1)
-        for oz in (3, -3):
-            relay_arrived(oz)
-            pass_on(0, oz, "R", 1)
-        for oz in (2, -2, 4, -4):
-            arrived(oz, 0)
-            pass_on(1, oz, "M", 1)
-        for oz in (6, -6):
-            arrived(oz, 0)
-            pass_on(1, oz, "M", 1)
-        for oz in (6, -6):
-            relay_arrived(oz)
-            pass_on(0, oz, "R", 1)
-        for oz, dy in HELD:
-            if dy or oz not in INNER:
-                arrived(oz, dy)
-
-    @pl.when(core == 0)
-    def _():
-        pass_on(0, 0, "M", 0)
-        for oz in (1, -1, 2, -2, 4, -4):
-            arrived(oz, 0)
-            pass_on(0, oz, "M", 0)
-        for oz, dy in HELD:
-            if dy or oz not in (0, 1, -1, 2, -2, 4, -4):
-                arrived(oz, dy)
-
-    xs[...] = buf[:, 0].astype(F32).reshape(xs.shape).astype(BF16)
-    ys[...] = buf[:, 1].astype(F32).reshape(ys.shape).astype(BF16)
+    def arrived(oz, dy, j):
+        ref = side(buf.at[seq_at(-oz, dy), j], oz)
+        copy_to(ref, ref, zs_sem.at[0, 0], zr_sem.at[HELD.index((oz, dy)), j], across).wait_recv()
+
+    def relay_arrived(oz, j):
+        ref = relay.at[RELAYED.index(oz), j]
+        copy_to(ref, ref, zs_sem.at[0, 0], rr_sem.at[RELAYED.index(oz), j], across).wait_recv()
+
+    def relay_blocks(c):
+        def stage(j, offsets):
+            for owner in ((1, 0) if c else (0,)):
+                for oz in offsets:
+                    if carrier(owner, oz) != c:
+                        continue
+                    if owner == c:
+                        arrived(oz, 0, j)
+                    else:
+                        relay_arrived(oz, j)
+                    pass_on(owner, oz, j, c)
+        for j in (0, 1):
+            pass_on(c, 0, j, c)
+        stage(0, (3, -3))
+        stage(0, (1, -1))
+        stage(1, (3, -3))
+        stage(1, (1, -1))
+        stage(0, (2, -2, 4, -4))
+        stage(0, (6, -6))
+        stage(1, (2, -2, 4, -4))
+        stage(1, (6, -6))
+        leaves_complete(c, 0)
+
+    def leaves_complete(c, j):
+        for oz, dy in sorted(HELD, key=lambda h: abs(h[0]) + h[1]):
+            if dy or oz not in INNER or carrier(c, oz) != c:
+                arrived(oz, dy, j)
+
+    on_cores(relay_blocks)
     for c in loads[2:]:
         c.wait()
+    xs[...] = buf[:, 0].astype(F32).reshape(xs.shape).astype(BF16)
 
     half = xs.shape[0] // 2
     mine = pl.ds(pl.multiple_of(core * half, half), half)
@@ -229,10 +224,13 @@
 
     chips = slabs.shape[1]
     share = half // chips
-    on_cores(all_ready)
-    for k in range(3):
+    def to_mate(k):
         far[k] = product(k, theirs)
         send(far.at[k], got.at[k], cs_sem.at[k], cr_sem.at[k], mate)
+
+    on_cores(all_ready)
+    to_mate(0)
+    to_mate(1)
     own[0] = product(0, mine)
     for k in range(3):
         copy_to(far.at[k], got.at[k], cs_sem.at[k], cr_sem.at[k], mate).wait_recv()
@@ -243,14 +241,20 @@
             chip = chip_at(a, b)
             send(slabs.at[k, chip], landed.at[i, k], ts_sem.at[i, k], tr_sem.at[i, k],
                  (s, chip * 2 + core))
-        if k < 2:
-            own[k + 1] = product(k + 1, mine)
+        if k == 0:
+            own[1] = product(1, mine)
+        if k == 1:
+            on_cores(lambda c: leaves_complete(c, 1))
+            ys[...] = buf[:, 1].astype(F32).reshape(ys.shape).astype(BF16)
+            to_mate(2)
+            own[2] = product(2, mine)
+    done()
     me = chip_at(0, 0)
     at = core * chips + me
     sums = []
     for k in range(3):
         total = own[k, pl.ds(pl.multiple_of(me * share, share), share), :]
-        for i in range(len(others)):
+        for i in reversed(range(len(others))):
             copy_to(slabs.at[k, 0], landed.at[i, k], ts_sem.at[i, k], tr_sem.at[i, k], mate).wait_recv()
             total = total + landed[i, k].astype(F32)
         sums.append(total)
@@ -274,13 +278,13 @@
     from_chips = [chip_at(-a, b) for a, b in others] + [me]
 
     def hand_over_units(late):
-        for i in range(len(others)):
+        for i in reversed(range(len(others))):
             ref = units_of(core * chips + from_chips[i], late)
             copy_to(ref, ref, as_sem.at[i, late], ar_sem.at[i, late], mate).wait_recv()
             send(ref, ref, bs_sem.at[i, late], br_sem.at[i, late], mate)
 
     def units_complete(late):
-        for i, chip in enumerate(from_chips):
+        for i, chip in reversed(list(enumerate(from_chips))):
             ref = units_of((1 - core) * chips + chip, late)
             copy_to(ref, ref, bs_sem.at[i, late], br_sem.at[i, late], mate).wait_recv()
 
@@ -298,11 +302,6 @@
 
     leaves[...] = term.reshape(dxp.shape).astype(BF16)
     first = (((0,), (0,)), ((), ()))
-    wide = depth // 2
-
-    def side(ref, oz):
-        return ref.at[:, pl.ds(0, wide)] if oz == 8 else ref.at[:, pl.ds(wide, wide)] if oz == -8 else ref
-
     def send_up(key, by):
         c, oz, dy, kind = key
         up, dz, _ = UP[key]
@@ -318,7 +317,8 @@
     def collected(c, oz):
         kind = "R" if carrier(c, oz) != c else "M"
         value = jnp.zeros((rows, depth), F32) if kind == "R" else dxp[seq_at(-oz)]
-        for dz, dy, to in inward(c, oz):
+        edges = inward(c, oz)
+        for dz, dy, to in sorted(edges, key=lambda e: abs(e[0])) if oz == 0 else edges[::-1]:
             key = (c, oz + dz, dy, to)
             if key in INNER_KEYS:
                 n = INNER_KEYS.index(key)
@@ -350,32 +350,39 @@
             send_up(key, c)
 
     def middle(c):
-        for oz in (4, -4, 2, -2, 1, -1):
+        for oz in (4, -4, 2, -2):
             forward(c, oz, c)
 
+    def inner(c):
+        for oz in (1, -1):
+            forward(c, oz, c)
+
     def outer(c):
-        for oz in (6, -6):
-            for b in ((1, 0) if c else ()):
+        for b in ((1, 0) if c else ()):
+            for oz in (6, -6):
                 forward(b, oz, c)
 
+    def three(c):
+        for b in ((1, 0) if c else ()):
+            for oz in (3, -3):
+                forward(b, oz, c)
+
     def finish(c):
-        for oz in (3, -3):
-            for b in ((1, 0) if c else ()):
-                forward(b, oz, c)
         dx_ref[...] = collected(c, 0).astype(BF16)
 
     on_cores(start_leaves)
+    on_cores(outer)
+    on_cores(middle)
+    on_cores(inner)
     hand_over_units(1)
     gg[...] = lax.dot_general(gate_unit, xs[...], first, preferred_element_type=F32)
-    on_cores(middle)
-    on_cores(outer)
     ug[...] = lax.dot_general(up_unit, xs[...], first, preferred_element_type=F32)
     units_complete(1)
     dg[...] = lax.dot_general(act[:, 0].reshape(tokens, units), ys[...], first,
                               preferred_element_type=F32)
+    on_cores(three)
+    done()
     on_cores(finish)
-
-    done()
 
 
 def write_out(dx, gg, ug, dg, dx_out, gg_out, ug_out, dg_out, staged, sem):
@@ -427,7 +434,7 @@
                 vmem((2 * nz, rows, depth), BF16), vmem((len(LEAF_KEYS), rows, depth), BF16),
                 vmem((len(INNER_KEYS), rows, depth), F32), vmem((len(INNER_KEYS), rows, depth), F32),
                 pltpu.SemaphoreType.REGULAR, dma((5,)),
-                dma((len(EDGES),)), dma((len(HELD),)), dma((4,)),
+                dma((len(EDGES), 2)), dma((len(HELD), 2)), dma((4, 2)),
                 dma((3,)), dma((3,)),
                 dma((7, 3)), dma((7, 3)), dma((7, 2)), dma((7, 2)), dma((8, 2)), dma((8, 2)),
                 dma((len(LEAF_KEYS),)), dma((len(LEAF_KEYS),)),

time: 60.1 us -> 59.3 us (0.987)
  Pallas kernels: 59.2 us -> 58.4 us
    pallas_call x1, Pallas kernels: 57.6 us -> 56.8 us  [per_device(): pl.pallas_call(lambda *refs: kernel(nz, nx, *refs), out_shape=(vmem((rows...]
where the time goes in v4:
time: 59.3 us; the launch traced here: 59 us
  Pallas kernels  58.4 us (98%)
  between operations  0.64 us (1%)
    pallas_call x1, Pallas kernels, per_device(): pl.pallas_call(lambda *refs: kernel(nz, nx, *refs), out_shape=(vmem((rows...  56.8 us
    pallas_call x1, Pallas kernels, per_device(): pl.pallas_call(write_out, out_shape=(jax.ShapeDtypeStruct((groups, local,...  1.6 us

profile of v4, /device:TPU:1, one launch (start us, length us, event | category | flops | bytes accessed | tf_op | source)
XLA Modules:
  0.0 59.0 jit_solution(17923249424657101277)
XLA Ops:
  0.6 56.8 %shard_map.84 = (bf16[8,512]{1,0:T(8,128)(2,1)S(1)}, f32[464,512]{1,0:T(8,128)S(1)}, f32[464,512]{1,0:T(8,128)S(1)}, f32[464,512]{1,0:T(8,128)S(1)}) custom-call(bf16[2,4,512]{2,1,0:T(4,128)(2,1)} %refs_0_.1, bf16[2,4,512]{2,1,0:T(4,128)(2,1)} %refs_1_.1, bf16[464,512]{1,0:T(8,128)(2,1)} %bitcast.4, bf16[464,512]{1,0:T(8,128)(2,1)} %bitcast.5, ...), custom_call_target="tpu_custom_call" | custom-call | tf_op jit(solution)/shard_map/pallas_call | solution.py:415
  57.4 1.6 %shard_map.85 = (bf16[2,4,512]{2,1,0:T(4,128)(2,1)}, f32[464,512]{1,0:T(8,128)}, f32[464,512]{1,0:T(8,128)}, f32[464,512]{1,0:T(8,128)}) custom-call(bf16[8,512]{1,0:T(8,128)(2,1)S(1)} %get-tuple-element.12.dx, f32[464,512]{1,0:T(8,128)S(1)} %get-tuple-element.13.gg, f32[464,512]{1,0:T(8,128)S(1)} %get-tuple-element.14.ug, f32[464,512]{1,0:T(8,128)S(1)} %get-tuple-element.15.dg), custom_call_target="tpu_custom_call" | custom-call | tf_op jit(solution)/shard_map/pallas_call | solution.py:448

commit v5 on v4

--- a/solution.py
+++ b/solution.py
@@ -158,9 +158,11 @@
     def side(ref, oz):
         return ref.at[:, pl.ds(0, wide)] if oz == 8 else ref.at[:, pl.ds(wide, wide)] if oz == -8 else ref
 
-    def pass_on(c, oz, j, by):
+    def pass_on(c, oz, j, by, lengths=(0, 1, 2, 3)):
         relays = carrier(c, oz) != c
         for dz, dy, to in onward(c, oz):
+            if abs(dz) not in lengths:
+                continue
             n = EDGES.index((c, oz, dz, dy, to))
             far = oz + dz
 
@@ -182,15 +184,17 @@
 
     def relay_blocks(c):
         def stage(j, offsets):
-            for owner in ((1, 0) if c else (0,)):
-                for oz in offsets:
-                    if carrier(owner, oz) != c:
-                        continue
-                    if owner == c:
-                        arrived(oz, 0, j)
-                    else:
-                        relay_arrived(oz, j)
-                    pass_on(owner, oz, j, c)
+            here = [(owner, oz) for owner in ((1, 0) if c else (0,)) for oz in offsets
+                    if carrier(owner, oz) == c]
+            for owner, oz in here:
+                if owner == c:
+                    arrived(oz, 0, j)
+                else:
+                    relay_arrived(oz, j)
+                pass_on(owner, oz, j, c, (3,) if abs(oz) == 3 else (0, 1, 2, 3))
+            for owner, oz in here:
+                if abs(oz) == 3:
+                    pass_on(owner, oz, j, c, (0, 1))
         for j in (0, 1):
             pass_on(c, 0, j, c)
         stage(0, (3, -3))

time: 59.3 us -> 59.6 us (level)
  no operation moved by 1% of the time
where the time goes in v5:
time: 59.6 us; the launch traced here: 59.4 us
  Pallas kernels  58.8 us (99%)
  between operations  0.64 us (1%)
    pallas_call x1, Pallas kernels, per_device(): pl.pallas_call(lambda *refs: kernel(nz, nx, *refs), out_shape=(vmem((rows...  57.2 us
    pallas_call x1, Pallas kernels, per_device(): pl.pallas_call(write_out, out_shape=(jax.ShapeDtypeStruct((groups, local,...  1.6 us

profile of v5, /device:TPU:1, one launch (start us, length us, event | category | flops | bytes accessed | tf_op | source)
XLA Modules:
  0.0 59.4 jit_solution(5360489695567444720)
XLA Ops:
  0.6 57.2 %shard_map.84 = (bf16[8,512]{1,0:T(8,128)(2,1)S(1)}, f32[464,512]{1,0:T(8,128)S(1)}, f32[464,512]{1,0:T(8,128)S(1)}, f32[464,512]{1,0:T(8,128)S(1)}) custom-call(bf16[2,4,512]{2,1,0:T(4,128)(2,1)} %refs_0_.1, bf16[2,4,512]{2,1,0:T(4,128)(2,1)} %refs_1_.1, bf16[464,512]{1,0:T(8,128)(2,1)} %bitcast.4, bf16[464,512]{1,0:T(8,128)(2,1)} %bitcast.5, ...), custom_call_target="tpu_custom_call" | custom-call | tf_op jit(solution)/shard_map/pallas_call | solution.py:419
  57.8 1.6 %shard_map.85 = (bf16[2,4,512]{2,1,0:T(4,128)(2,1)}, f32[464,512]{1,0:T(8,128)}, f32[464,512]{1,0:T(8,128)}, f32[464,512]{1,0:T(8,128)}) custom-call(bf16[8,512]{1,0:T(8,128)(2,1)S(1)} %get-tuple-element.12.dx, f32[464,512]{1,0:T(8,128)S(1)} %get-tuple-element.13.gg, f32[464,512]{1,0:T(8,128)S(1)} %get-tuple-element.14.ug, f32[464,512]{1,0:T(8,128)S(1)} %get-tuple-element.15.dg), custom_call_target="tpu_custom_call" | custom-call | tf_op jit(solution)/shard_map/pallas_call | solution.py:452
